TPU v7x, 16 devices: a whole 2x2x2 slice. The times are simulated.
16 devices in a mesh: yz: 4 (over z, y), x: 4 (over x, core).
Axes of the slice: x: 2, y: 2, z: 2, core: 2. Of those that a mesh axis runs over, the one named last changes fastest.
Arguments:
- h: bfloat16 [128, 2048], P(None, ('x', 'yz'))
- g: bfloat16 [2, 2048], P(None, ('x', 'yz'))
- wq: bfloat16 [2, 2048, 2048], P(None, 'x', 'yz')
- wk: bfloat16 [2, 2048, 2048], P(None, 'x', 'yz')
- wv: bfloat16 [2, 2048, 2048], P(None, 'x', 'yz')
- w_in: bfloat16 [2, 2048, 8192], P(None, 'x', 'yz')
- wo: bfloat16 [2, 2048, 2048], P(None, 'yz', 'x')
- w_out: bfloat16 [2, 8192, 2048], P(None, 'yz', 'x')
- k_cache: bfloat16 [2, 128, 16, 512, 128], P(None, None, ('yz', 'x'))
- v_cache: bfloat16 [2, 128, 16, 512, 128], P(None, None, ('yz', 'x'))
- lens: int32 [128], replicated
Outputs:
- output 1: bfloat16 [128, 2048], P(None, ('x', 'yz'))
- output 2: bfloat16 [2, 128, 16, 128], P(None, None, ('yz', 'x'))
- output 3: bfloat16 [2, 128, 16, 128], P(None, None, ('yz', 'x'))
All inputs are finite; a program needn't handle non-finite values.
Results may differ from a plain program's by a relative error of at most 0.0191147.
Values are sent between devices in bfloat16 or wider.
A program may use at most 1 GiB of HBM per device.

v0:
```python
import jax
import jax.numpy as jnp
from jax import lax
from jax.sharding import PartitionSpec as P

EPS = 1e-6


def _rope(t, lens):
    half = t.shape[-1] // 2
    inv = 10000.0 ** (-jnp.arange(half, dtype=jnp.float32) / half)
    ang = lens.astype(jnp.float32)[:, None, None] * inv
    c, s = jnp.cos(ang), jnp.sin(ang)
    tf = t.astype(jnp.float32)
    a, b = tf[..., :half], tf[..., half:]
    return jnp.concatenate([a * c - b * s, b * c + a * s], axis=-1).astype(jnp.bfloat16)


def _attend(q, kc, vc, k, v, lens):
    scale = q.shape[-1] ** -0.5
    s = jnp.einsum('bhd,bhsd->bhs', q, kc, preferred_element_type=jnp.float32) * scale
    pos = jnp.arange(kc.shape[2])
    s = jnp.where(pos[None, None, :] < lens[:, None, None], s, -jnp.inf)
    sn = jnp.einsum('bhd,bhd->bh', q, k, preferred_element_type=jnp.float32) * scale
    m = jnp.maximum(jnp.max(s, axis=-1), sn)
    p = jnp.exp(s - m[..., None])
    pn = jnp.exp(sn - m)
    den = jnp.sum(p, axis=-1) + pn
    o = jnp.einsum('bhs,bhsd->bhd', p.astype(jnp.bfloat16), vc, preferred_element_type=jnp.float32)
    o = o + pn[..., None] * v.astype(jnp.float32)
    return (o / den[..., None]).astype(jnp.bfloat16)


def solution(mesh):
    X = mesh.shape['x']
    Y = mesh.shape['yz']
    act = P(None, ('x', 'yz'))
    w_first = P(None, 'x', 'yz')
    w_second = P(None, 'yz', 'x')
    cache = P(None, None, ('yz', 'x'), None, None)
    new = P(None, None, ('yz', 'x'), None)

    def body(h, g, wq, wk, wv, w_in, wo, w_out, kc, vc, lens):
        bsz = h.shape[0]
        hl, dh = kc.shape[2], kc.shape[4]
        hdn = hl * dh
        e_total = h.shape[1] * X * Y
        ks, vs = [], []
        for l in range(wq.shape[0]):
            hf = h.astype(jnp.float32)
            ss = lax.psum(jnp.sum(hf * hf, axis=-1, keepdims=True), ('yz', 'x'))
            x = (hf * lax.rsqrt(ss / e_total + EPS) * g[l].astype(jnp.float32)).astype(jnp.bfloat16)
            xg = lax.all_gather(x, 'yz', axis=1, tiled=True)
            parts = [jnp.dot(xg, w[l], preferred_element_type=jnp.float32).astype(jnp.bfloat16).reshape(bsz, X, -1)
                     for w in (wq, wk, wv, w_in)]
            r = lax.psum_scatter(jnp.concatenate(parts, axis=2), 'x', scatter_dimension=1, tiled=True)[:, 0]
            q = _rope(r[:, :hdn].reshape(bsz, hl, dh), lens)
            k = _rope(r[:, hdn:2 * hdn].reshape(bsz, hl, dh), lens)
            v = r[:, 2 * hdn:3 * hdn].reshape(bsz, hl, dh)
            f = jax.nn.gelu(r[:, 3 * hdn:].astype(jnp.float32), approximate=True).astype(jnp.bfloat16)
            o = _attend(q, kc[l], vc[l], k, v, lens).reshape(bsz, hdn)
            ga = lax.all_gather(jnp.concatenate([o, f], axis=1), 'x', axis=1)
            og = ga[:, :, :hdn].reshape(bsz, -1)
            fg = ga[:, :, hdn:].reshape(bsz, -1)
            yp = (jnp.dot(og, wo[l], preferred_element_type=jnp.float32)
                  + jnp.dot(fg, w_out[l], preferred_element_type=jnp.float32)).astype(jnp.bfloat16)
            y = lax.psum_scatter(yp, 'yz', scatter_dimension=1, tiled=True)
            h = (hf + y.astype(jnp.float32)).astype(jnp.bfloat16)
            ks.append(k)
            vs.append(v)
        return h, jnp.stack(ks), jnp.stack(vs)

    return jax.shard_map(
        body, mesh=mesh,
        in_specs=(act, act, w_first, w_first, w_first, w_first, w_second, w_second, cache, cache, P(None)),
        out_specs=(act, new, new), check_vma=False)
```

profile of v0, /device:TPU:0, one launch (start us, length us, event | category | flops | bytes accessed | tf_op | source)
XLA Modules:
  0.0 261.7 jit_solution(3530140025133160434)
XLA Ops:
  7.2 0.9 fusion.118
  8.1 34.7 %psum.14 = f32[128,1]{0,1:T(1,128)S(1)} all-reduce(f32[128,1]{0,1:T(1,128)S(1)} %bitcast.242), channel_id=1, replica_groups=mesh['yz'=4,'x'=4] {'yz','x'}, use_global_device_ids=true, to_apply=%region_1.0 | all-reduce | flops 128 | bytes 1024 | tf_op jit(solution)/shard_map/psum | solution.py:51
  42.8 0.7 bitcast_convert_fusion.1
  43.5 0.8 fusion.120
  44.3 9.2 %all_gather.18 = bf16[128,512]{1,0:T(8,128)(2,1)S(1)} all-gather(bf16[128,128]{1,0:T(8,128)(2,1)S(1)} %fusion.120), channel_id=1, replica_groups=mesh['yz'=4,'x'=4] {'yz'}, dimensions={1}, use_global_device_ids=true | all-gather | bytes 163840 | tf_op jit(solution)/shard_map/all_gather | solution.py:53
  53.6 1.3 fusion.36
  54.8 1.3 fusion.35
  56.1 1.3 fusion.34
  57.5 2.0 convolution_convert_fusion.1
  59.6 1.0 pad_maximum_fusion
  60.7 19.3 %reduce-scatter.9.cloned.1.call-done = bf16[128,1,896]{2,0,1:T(8,128)(2,1)} async-done(((bf16[128,4,896]{2,0,1:T(8,128)(2,1)}), bf16[128,1,896]{2,0,1:T(8,128)(2,1)}) %reduce-scatter.9.cloned.1.call-update) | async-done | bytes 229392 | tf_op jit(solution)/shard_map/reduce_scatter | solution.py:56
  80.1 1.0 fusion.63
  81.1 0.8 slice_bitcast_fusion.5
  81.9 0.3 fusion.107
  82.3 10.2 %fusion.6 = f32[128,1,512]{2,1,0:T(1,128)S(1)} fusion(bf16[2,128,1,512,128]{4,3,2,1,0:T(8,128)(2,1)} %param.19, bf16[128,128,1]{1,0,2:T(8,128)(2,1)S(1)} %fusion.139), kind=kOutput, calls=%fused_computation.6 | convolution fusion | flops 16777216 | bytes 17072128 | tf_op jit(solution)/shard_map/bhd,bhsd->bhs/dot_general | solution.py:21
  92.9 0.2 fusion.74
  93.1 7.0 %fusion.4 = f32[128,1,128]{2,1,0:T(1,128)S(1)} fusion(bf16[2,128,1,512,128]{4,3,2,1,0:T(8,128)(2,1)} %param.20, bf16[128,512,1]{1,0,2:T(8,128)(2,1)S(1)} %get-tuple-element.10), kind=kOutput, calls=%fused_computation.4 | convolution fusion | flops 16777216 | bytes 16973824 | tf_op jit(solution)/shard_map/bhs,bhsd->bhd/dot_general | solution.py:29
  100.2 0.9 divide_convert_fusion.1
  101.2 7.2 %all-gather = bf16[128,2560]{1,0:T(8,128)(2,1)S(1)} all-gather(bf16[128,640]{1,0:T(8,128)(2,1)S(1)} %pad_maximum_fusion.2), channel_id=2, replica_groups=mesh['yz'=4,'x'=4] {'x'}, dimensions={1}, use_global_device_ids=true | all-gather | bytes 819200 | tf_op jit(solution)/shard_map/all_gather | solution.py:62
  108.9 0.2 fusion.45
  109.2 2.0 fusion.31
  111.2 0.7 copy.54
  112.0 21.2 %reduce-scatter.13.cloned.1.call-done = bf16[128,128]{1,0:T(8,128)(2,1)} async-done(((bf16[512,128]{1,0:T(8,128)(2,1)}), bf16[128,128]{1,0:T(8,128)(2,1)}) %reduce-scatter.13.cloned.1.call-update) | async-done | bytes 32784
  133.2 0.9 copy.55
  134.2 31.8 %psum.15 = f32[128,1]{0,1:T(1,128)S(1)} all-reduce(f32[128,1]{0,1:T(1,128)S(1)} %bitcast.243), channel_id=1, replica_groups=mesh['yz'=4,'x'=4] {'yz','x'}, use_global_device_ids=true, to_apply=%region_7.8 | all-reduce | flops 128 | bytes 1024 | tf_op jit(solution)/shard_map/psum | solution.py:51
  166.1 9.2 %all_gather.21 = bf16[128,512]{1,0:T(8,128)(2,1)S(1)} all-gather(bf16[128,128]{1,0:T(8,128)(2,1)S(1)} %fusion.124), channel_id=1, replica_groups=mesh['yz'=4,'x'=4] {'yz'}, dimensions={1}, use_global_device_ids=true | all-gather | bytes 163840 | tf_op jit(solution)/shard_map/all_gather | solution.py:53
  175.4 0.2 fusion.39
  175.6 0.2 fusion.38
  175.8 1.3 fusion.37
  177.1 2.0 convolution_convert_fusion
  179.3 1.0 pad_maximum_fusion.1
  180.4 0.2 reduce-scatter.15.cloned.1.call-start
  180.6 20.1 %reduce-scatter.11.cloned.1.call-done = bf16[128,1,896]{2,0,1:T(8,128)(2,1)} async-done(((bf16[128,4,896]{2,0,1:T(8,128)(2,1)}), bf16[128,1,896]{2,0,1:T(8,128)(2,1)}) %reduce-scatter.11.cloned.1.call-update) | async-done | bytes 229392 | tf_op jit(solution)/shard_map/reduce_scatter | solution.py:56
  200.7 1.0 fusion.69
  201.7 0.8 slice_bitcast_fusion.4
  202.5 0.3 fusion.115
  202.9 10.2 %fusion.2 = f32[128,1,512]{2,1,0:T(1,128)S(1)} fusion(bf16[2,128,1,512,128]{4,3,2,1,0:T(8,128)(2,1)} %param.19, bf16[128,128,1]{1,0,2:T(8,128)(2,1)S(1)} %fusion.138), kind=kOutput, calls=%fused_computation.2 | convolution fusion | flops 16777216 | bytes 17072128 | tf_op jit(solution)/shard_map/bhd,bhsd->bhs/dot_general | solution.py:21
  213.7 7.0 %fusion = f32[128,1,128]{2,1,0:T(1,128)S(1)} fusion(bf16[2,128,1,512,128]{4,3,2,1,0:T(8,128)(2,1)} %param.20, bf16[128,512,1]{1,0,2:T(8,128)(2,1)S(1)} %get-tuple-element.8), kind=kOutput, calls=%fused_computation | convolution fusion | flops 16777216 | bytes 16973824 | tf_op jit(solution)/shard_map/bhs,bhsd->bhd/dot_general | solution.py:29
  220.8 0.9 divide_convert_fusion
  221.7 7.2 %all-gather.1 = bf16[128,2560]{1,0:T(8,128)(2,1)S(1)} all-gather(bf16[128,640]{1,0:T(8,128)(2,1)S(1)} %pad_maximum_fusion.3), channel_id=3, replica_groups=mesh['yz'=4,'x'=4] {'x'}, dimensions={1}, use_global_device_ids=true | all-gather | bytes 819200 | tf_op jit(solution)/shard_map/all_gather | solution.py:62
  229.4 0.2 fusion.40
  229.6 2.0 fusion.28
  231.7 0.7 copy.56
  232.5 0.6 pad_maximum_fusion.4
  233.1 0.7 maximum_maximum_fusion
  233.8 19.8 %reduce-scatter.15.cloned.1.call-done = bf16[128,128]{1,0:T(8,128)(2,1)} async-done(((bf16[512,128]{1,0:T(8,128)(2,1)}), bf16[128,128]{1,0:T(8,128)(2,1)}) %reduce-scatter.15.cloned.1.call-update) | async-done | bytes 32784
  253.6 0.9 copy.57
  254.5 0.6 fusion.125
  (51 shorter events, 2.8 us)
Async XLA Ops:
  7.2 72.9 %reduce-scatter.9.cloned.1.call-start = ((), (), s32[]{:S(2)}) async-start(), calls=%async_computation.4 | async-start | bytes 1146880 | tf_op jit(solution)/shard_map/reduce_scatter | solution.py:56
  56.1 4.6 %copy-start.4 = (s32[128]{0:T(128)S(1)}, s32[128]{0:T(128)}, u32[]{:S(2)}) copy-start(s32[128]{0:T(128)} %param.21) | copy-start | bytes 1540
  60.7 72.5 %reduce-scatter.13.cloned.1.call-start = ((), (), s32[]{:S(2)}) async-start(), calls=%async_computation.6 | async-start | bytes 163840
  100.2 8.7 %copy-start = (bf16[2,512,512]{2,1,0:T(8,128)(2,1)S(1)}, bf16[2,512,512]{2,1,0:T(8,128)(2,1)}, u32[]{:S(2)}) copy-start(bf16[2,512,512]{2,1,0:T(8,128)(2,1)} %param.17) | copy-start | bytes 3145732
  108.4 25.7 %copy-start.3 = (bf16[128,128]{1,0:T(8,128)(2,1)S(1)}, bf16[128,128]{1,0:T(8,128)(2,1)}, u32[]{:S(2)}) copy-start(bf16[128,128]{1,0:T(8,128)(2,1)} %param.11) | copy-start | bytes 98308
  108.4 67.0 %copy-start.1 = (bf16[2,512,512]{2,1,0:T(8,128)(2,1)S(1)}, bf16[2,512,512]{2,1,0:T(8,128)(2,1)}, u32[]{:S(2)}) copy-start(bf16[2,512,512]{2,1,0:T(8,128)(2,1)} %param.15) | copy-start | bytes 3145732
  108.8 66.8 %copy-start.2 = (bf16[2,512,512]{2,1,0:T(8,128)(2,1)S(1)}, bf16[2,512,512]{2,1,0:T(8,128)(2,1)}, u32[]{:S(2)}) copy-start(bf16[2,512,512]{2,1,0:T(8,128)(2,1)} %param.14) | copy-start | bytes 3145732
  112.0 88.7 %reduce-scatter.11.cloned.1.call-start = ((), (), s32[]{:S(2)}) async-start(), calls=%async_computation.5 | async-start | bytes 1146880 | tf_op jit(solution)/shard_map/reduce_scatter | solution.py:56
  180.4 73.3 %reduce-scatter.15.cloned.1.call-start = ((), (), s32[]{:S(2)}) async-start(), calls=%async_computation.7 | async-start | bytes 163840
Sparse Core Ops, SparseCore 0:
  60.8 19.2 reduce-scatter.8
  112.1 21.0 reduce-scatter.12
  180.5 20.1 reduce-scatter.10
  232.6 20.9 reduce-scatter.14
where the time goes:
time: 263 us; the launch traced here: 262 us
  blocking collectives  99.4 us (38%)
  waiting for transfers between devices  80.5 us (31%)
  matrix products  48.6 us (18%)
  other arithmetic  14.3 us (5%)
  between operations  14.2 us (5%)
  local copies, waits for them, and re-layouts  4.42 us (2%)
    psum x2, blocking collectives, body(): ss = lax.psum(jnp.sum(hf * hf, axis=-1, keepdims=True), ('yz', 'x'))  66.5 us
    unnamed x6, waiting for transfers between devices  41 us
    reduce_scatter x2, waiting for transfers between devices, body(): lax.psum_scatter(jnp.concatenate(parts, axis=2), 'x', scatter_dimension=1...  39.4 us
    dot_general x2, matrix products, _attend(): jnp.einsum('bhd,bhsd->bhs', q, kc, preferred_element_type=jnp.float32)  20.4 us
    all_gather x2, blocking collectives, body(): xg = lax.all_gather(x, 'yz', axis=1, tiled=True)  18.4 us
    all_gather x2, blocking collectives, body(): ga = lax.all_gather(jnp.concatenate([o, f], axis=1), 'x', axis=1)  14.4 us
    dot_general x2, matrix products, _attend(): jnp.einsum('bhs,bhsd->bhd', p.astype(jnp.bfloat16), vc, preferred_element...  14.1 us
    dot_general x8, matrix products, body(): jnp.dot(xg, w[l], preferred_element_type=jnp.float32).astype(jnp.bfloat16)  9.64 us
  transfers between devices with their start and end apart: 4, of which 4 were waited for; matrix products, arithmetic and copies ran while one was open for 1% of the time, Pallas kernels for 0%

commit v1 on v0

v1 whole, which is shorter than its diff:
```python
import functools

import jax
import jax.numpy as jnp
import numpy as np
from jax import lax
from jax.experimental import pallas as pl
from jax.experimental.pallas import tpu as pltpu
from jax.sharding import PartitionSpec as P

EPS = 1e-6
MESH = pl.DeviceIdType.MESH
F32 = jnp.float32
BF16 = jnp.bfloat16

L = 2
B = 128
D = 128
S = 512
NX = 4
NY = 4
E = 2048
G = 16
NG = B // G


def _dot(a, b):
    return jnp.dot(a, b, preferred_element_type=F32)


def _dot_t(a, b):
    return lax.dot_general(a, b, (((1,), (1,)), ((), ())), preferred_element_type=F32)


def _kernel(nch, h_in, g_in, wq_in, wk_in, wv_in, win_in, wo_in, wout_in, kc_in, vc_in, lens_in, inv_in,
            h_out, k_out, v_out,
            kbuf, vbuf, wq, wk, wv, win, wo, wout, gg, lrow, inv, cosb, sinb, lenb,
            hg, ssb, pf, pb, rq, sf, sb, xr, uf, ub, ur, usf, usb, ux, fb, og, zf, zb, zr,
            qv, kv, vv, hout,
            sem_in, sem_w, sem_k, sem_v, sem_o,
            s_send, s_recv, h_send, h_recv, g_send, g_recv, q_send, q_recv, qx_send, qx_recv,
            u_send, u_recv, f_send, f_recv, o_send, o_recv, y_send, y_recv):
    R = B // nch
    xi = lax.axis_index("x")
    yi = lax.axis_index("yz")
    c = lax.rem(xi, 2)
    xc = lax.div(xi, 2)
    partner = xi + 1 - 2 * c
    across = lax.rem(xi + 2, NX)
    sends = []

    def remote(src, dst, ss, rs, **dev):
        dev.setdefault("x", xi)
        dev.setdefault("yz", yi)
        cp = pltpu.make_async_remote_copy(src_ref=src, dst_ref=dst, send_sem=ss, recv_sem=rs,
                                          device_id=dev, device_id_type=MESH)
        cp.start()
        sends.append(cp)
        return cp

    def load(src, dst, sem):
        cp = pltpu.make_async_copy(src, dst, sem)
        cp.start()
        return cp

    in_h = load(h_in, hg.at[0, yi], sem_in.at[0])
    in_g = load(g_in, gg.at[yi], sem_in.at[1])
    in_l = load(lens_in, lrow, sem_in.at[2])
    in_i = load(inv_in, inv, sem_in.at[3])
    weights = (wq, wk, wv, win, wo, wout)
    sources = (wq_in, wk_in, wv_in, win_in, wo_in, wout_in)
    w_cp = {}

    def load_w(l, n):
        w_cp[l, n] = load(sources[n].at[l], weights[n].at[l], sem_w.at[l, n])

    for n in range(4):
        load_w(0, n)

    barrier = pltpu.get_barrier_semaphore()
    for dx in range(NX):
        for dy in range(NY):
            if dx or dy:
                pl.semaphore_signal(barrier, inc=1, device_id={"yz": lax.rem(yi + dy, NY), "x": lax.rem(xi + dx, NX)},
                                    device_id_type=MESH)
    pl.semaphore_wait(barrier, NX * NY - 1)

    eye = (lax.broadcasted_iota(jnp.int32, (R, B), 0) == lax.broadcasted_iota(jnp.int32, (R, B), 1))

    def send_stats(l, ch, hb):
        col = jnp.sum(hb * hb, axis=1, keepdims=True)
        row = jnp.sum(jnp.where(eye, col, 0.0), axis=0, keepdims=True)
        ssb[l, ch, 0] = row
        for dx in range(NX):
            for dy in range(NY):
                slot = dx * NY + dy
                if slot:
                    remote(ssb.at[l, ch, 0], ssb.at[l, ch, slot], s_send.at[l, ch, slot], s_recv.at[l, ch, slot],
                           x=lax.rem(xi + dx, NX), yz=lax.rem(yi + dy, NY))

    h_cp = {}

    def send_h(l, ch):
        rows = pl.ds(ch * R, R)
        h_cp[l, ch] = [remote(hg.at[l, yi, rows], hg.at[l, yi, rows], h_send.at[l, ch, d], h_recv.at[l, ch, d],
                              yz=lax.rem(yi + d, NY)) for d in (2, 1, 3)]

    in_h.wait()
    in_g.wait()
    g_cp = [remote(gg.at[yi], gg.at[yi], g_send.at[d], g_recv.at[d], yz=lax.rem(yi + d, NY)) for d in (1, 2, 3)]
    for ch in range(nch):
        hb = hg[0, yi, pl.ds(ch * R, R), :].astype(F32)
        send_stats(0, ch, hb)
        send_h(0, ch)

    def load_cache(l, grp):
        seqs = pl.ds(grp * G, G)
        pltpu.make_async_copy(kc_in.at[l, seqs], kbuf.at[seqs], sem_k.at[grp]).start()
        pltpu.make_async_copy(vc_in.at[l, seqs], vbuf.at[seqs], sem_v.at[grp]).start()

    for grp in range(NG):
        load_cache(0, grp)
    for n in (5, 4):
        load_w(0, n)
    for n in range(6):
        load_w(1, n)

    in_l.wait()
    in_i.wait()
    eye_b = (lax.broadcasted_iota(jnp.int32, (B, B), 0) == lax.broadcasted_iota(jnp.int32, (B, B), 1))
    lcol = jnp.sum(jnp.where(eye_b, lrow[...].astype(F32), 0.0), axis=1, keepdims=True)
    lenb[...] = jnp.broadcast_to(lcol, (B, D))
    ang = lcol * inv[...]
    cosb[...] = jnp.cos(ang)
    half = lax.broadcasted_iota(jnp.int32, (B, D), 1) < D // 2
    sn = jnp.sin(ang)
    sinb[...] = jnp.where(half, -sn, sn)

    waited = set()

    def need_w(l, *ns):
        for n in ns:
            if (l, n) not in waited:
                waited.add((l, n))
                w_cp[l, n].wait()

    q_cp, u_cp, x_cp, ux_cp, f_cp, o_cp, y_cp = {}, {}, {}, {}, {}, {}, {}

    def stage_in(l, ch):
        rows = pl.ds(ch * R, R)
        for cp in h_cp[l, ch]:
            cp.wait_recv()
        if l == 0 and ch == 0:
            for cp in g_cp:
                cp.wait_recv()
        for slot in range(1, NX * NY):
            pltpu.make_async_copy(ssb.at[l, ch, slot], ssb.at[l, ch, slot], s_recv.at[l, ch, slot]).wait()
        row = ssb[l, ch, 0]
        for slot in range(1, NX * NY):
            row = row + ssb[l, ch, slot]
        col = jnp.sum(jnp.where(eye, row, 0.0), axis=1, keepdims=True)
        r = lax.rsqrt(col / E + EPS)
        xs = []
        for j in range(NY):
            gj = gg[j, pl.ds(l, 1), :].astype(F32)
            xs.append((hg[l, j, rows, :].astype(F32) * r * gj).astype(BF16))
        x = jnp.concatenate(xs, axis=1)
        for t, w in enumerate((wq, wk, wv)):
            need_w(l, t)
            for n in range(2):
                acc = _dot(x, w[l, :, pl.ds(n * 256, 256)])
                for cc in range(2):
                    a = acc[:, cc * D:(cc + 1) * D]
                    pf[cc, t, n, rows, :] = a
                    pb[l, cc, t, n, rows, :] = a.astype(BF16)
            if t == 0:
                q_cp[l, ch, 0] = remote(pb.at[l, 1 - c, pl.ds(0, 1), :, rows], rq.at[l, pl.ds(0, 1), :, rows],
                                        q_send.at[l, ch, 0], q_recv.at[l, ch, 0], x=partner)
        q_cp[l, ch, 1] = remote(pb.at[l, 1 - c, pl.ds(1, 2), :, rows], rq.at[l, pl.ds(1, 2), :, rows],
                                q_send.at[l, ch, 1], q_recv.at[l, ch, 1], x=partner)
        reduce_qkv(l, ch, 0)
        need_w(l, 3)
        for n in range(8):
            acc = _dot(x, win[l, :, pl.ds(n * 256, 256)])
            cols = pl.ds((n % 4) * 256, 256)
            uf[n // 4, rows, cols] = acc
            ub[l, n // 4, rows, cols] = acc.astype(BF16)
        u_cp[l, ch] = remote(ub.at[l, 1 - c, rows], ur.at[l, rows], u_send.at[l, ch, 0], u_recv.at[l, ch, 0],
                             x=partner)
        reduce_qkv(l, ch, 1)

    def reduce_qkv(l, ch, part):
        rows = pl.ds(ch * R, R)
        ts = (0,) if part == 0 else (1, 2)
        q_cp[l, ch, part].wait_recv()
        for t in ts:
            for n in range(2):
                s = pf[c, t, n, rows, :] + rq[l, t, n, rows, :].astype(F32)
                sf[n, t, rows, :] = s
                sb[l, n, t, rows, :] = s.astype(BF16)
        span = pl.ds(ts[0], len(ts))
        x_cp[l, ch, part] = remote(sb.at[l, 1 - xc, span, rows], xr.at[l, span, rows],
                                   qx_send.at[l, ch, part], qx_recv.at[l, ch, part], x=across)

    def reduce_u(l, ch):
        rows = pl.ds(ch * R, R)
        u_cp[l, ch].wait_recv()
        us = uf[c, rows, :] + ur[l, rows, :].astype(F32)
        usf[rows, :] = us
        usb[l, rows, :] = us.astype(BF16)
        ux_cp[l, ch] = remote(usb.at[l, rows], ux.at[l, rows], u_send.at[l, ch, 1], u_recv.at[l, ch, 1], x=across)

    def rope(t, rows):
        tf = t.astype(F32)
        return (tf * cosb[rows, :] + pltpu.roll(tf, D // 2, 1) * sinb[rows, :]).astype(BF16)

    def stage_qkv(l, ch):
        rows = pl.ds(ch * R, R)
        x_cp[l, ch, 0].wait_recv()
        qv[rows, :] = rope((sf[xc, 0, rows, :] + xr[l, 0, rows, :].astype(F32)).astype(BF16), rows)
        x_cp[l, ch, 1].wait_recv()
        kv[l, rows, :] = rope((sf[xc, 1, rows, :] + xr[l, 1, rows, :].astype(F32)).astype(BF16), rows)
        vv[l, rows, :] = (sf[xc, 2, rows, :] + xr[l, 2, rows, :].astype(F32)).astype(BF16)

    rowid = lax.broadcasted_iota(jnp.int32, (G, D), 0)
    pos = lax.broadcasted_iota(jnp.int32, (G, S), 1).astype(F32)
    scale = D ** -0.5

    def attend(l, g0, g1):
        @pl.loop(g0, g1)
        def _(grp):
            base = grp * G
            rows = pl.ds(base, G)
            pltpu.make_async_copy(kc_in.at[l, rows], kbuf.at[rows], sem_k.at[grp]).wait()
            pltpu.make_async_copy(vc_in.at[l, rows], vbuf.at[rows], sem_v.at[grp]).wait()
            qf = qv[rows, :].astype(F32)
            s = jnp.zeros((G, S), F32)
            for i in range(0, G, 2):
                lhs = jnp.concatenate([jnp.where(rowid == i, qf, 0.0), jnp.where(rowid == i + 1, qf, 0.0)],
                                      axis=1).astype(BF16)
                s = s + _dot_t(lhs, jnp.concatenate([kbuf[base + i], kbuf[base + i + 1]], axis=1))
            s = jnp.where(pos < lenb[rows, :][:, :1], s * scale, -jnp.inf)
            kf = kv[l, rows, :].astype(F32)
            vf = vv[l, rows, :].astype(F32)
            s_new = jnp.sum(qf * kf, axis=1, keepdims=True) * scale
            m = jnp.maximum(jnp.max(s, axis=1, keepdims=True), s_new)
            p = jnp.exp(s - m)
            p_new = jnp.exp(s_new - m)
            den = jnp.sum(p, axis=1, keepdims=True) + p_new
            p = p.astype(BF16)
            o = p_new * vf
            for i in range(0, G, 2):
                t = _dot(p, jnp.concatenate([vbuf[base + i], vbuf[base + i + 1]], axis=1))
                o = o + jnp.where(rowid == i, t[:, :D], jnp.where(rowid == i + 1, t[:, D:], 0.0))
            og[l, xi, rows, :] = (o / den).astype(BF16)
            if l + 1 < L:
                load_cache(l + 1, grp)

    def send_o(l, ch):
        rows = pl.ds(ch * R, R)
        o_cp[l, ch] = [remote(og.at[l, xi, rows], og.at[l, xi, rows], o_send.at[l, ch, n], o_recv.at[l, ch, n], x=dst)
                       for n, dst in enumerate((across, lax.rem(partner + 2, NX), partner))]

    def stage_f(l, ch):
        rows = pl.ds(ch * R, R)
        ux_cp[l, ch].wait_recv()
        u = (usf[rows, :] + ux[l, rows, :].astype(F32)).astype(BF16)
        fb[l, c, rows, :] = jax.nn.gelu(u.astype(F32), approximate=True).astype(BF16)
        f_cp[l, ch] = remote(fb.at[l, c, rows], fb.at[l, c, rows], f_send.at[l, ch], f_recv.at[l, ch], x=partner)

    def stage_mlp(l, ch):
        rows = pl.ds(ch * R, R)
        f_cp[l, ch].wait_recv()
        need_w(l, 5)
        f = jnp.concatenate([fb[l, 0, rows, :], fb[l, 1, rows, :]], axis=1)
        for n in range(2):
            zf[pl.ds(2 * n, 1), rows, :], zf[pl.ds(2 * n + 1, 1), rows, :] = (
                a[None] for a in jnp.split(_dot(f, wout[l, :, pl.ds(n * 256, 256)]), 2, axis=1))

    def stage_out(l, ch):
        rows = pl.ds(ch * R, R)
        need_w(l, 4)
        for cp in o_cp[l, ch]:
            cp.wait_recv()
        o = jnp.concatenate([og[l, j, rows, :] for j in range(NX)], axis=1)
        for n in range(2):
            acc = _dot(o, wo[l, :, pl.ds(n * 256, 256)])
            for m in range(2):
                a = acc[:, m * D:(m + 1) * D] + zf[2 * n + m, rows, :]
                zf[2 * n + m, rows, :] = a
                zb[l, 2 * n + m, rows, :] = a.astype(BF16)
        y_cp[l, ch] = []
        for d in (2, 1, 3):
            to = lax.rem(yi + d, NY)
            y_cp[l, ch].append(remote(zb.at[l, to, rows], zr.at[l, d - 1, rows], y_send.at[l, ch, d],
                                      y_recv.at[l, ch, d], yz=to))

    out_cps = []

    def stage_h(l, ch):
        rows = pl.ds(ch * R, R)
        for cp in y_cp[l, ch]:
            cp.wait_recv()
        y = zf[yi, rows, :]
        for d in range(NY - 1):
            y = y + zr[l, d, rows, :].astype(F32)
        hn = (hg[l, yi, rows, :].astype(F32) + y.astype(BF16).astype(F32)).astype(BF16)
        if l + 1 < L:
            hg[l + 1, yi, rows, :] = hn
            send_stats(l + 1, ch, hn.astype(F32))
            send_h(l + 1, ch)
        else:
            hout[rows, :] = hn
            out_cps.append(load(hout.at[rows], h_out.at[rows], sem_o.at[0, ch]))

    gpc = NG // nch
    for l in range(L):
        for ch in range(nch):
            stage_in(l, ch)
            reduce_u(l, ch)
            stage_qkv(l, ch)
        out_cps.append(load(kv.at[l], k_out.at[l], sem_o.at[1, l]))
        out_cps.append(load(vv.at[l], v_out.at[l], sem_o.at[2, l]))
        for ch in range(nch):
            attend(l, ch * gpc, (ch + 1) * gpc)
            send_o(l, ch)
            stage_f(l, ch)
            stage_mlp(l, ch)
            stage_out(l, ch)
        for ch in range(nch):
            stage_h(l, ch)
    for cp in out_cps:
        cp.wait()
    for cp in sends:
        cp.wait_send()


def solution(mesh):
    nch = 1
    act = P(None, ('x', 'yz'))
    w_first = P(None, 'x', 'yz')
    w_second = P(None, 'yz', 'x')
    cache = P(None, None, ('yz', 'x'), None, None)
    new = P(None, None, ('yz', 'x'), None)
    inv_half = 10000.0 ** (-np.arange(D // 2, dtype=np.float64) / (D // 2))
    inv_np = np.concatenate([inv_half, inv_half]).astype(np.float32)[None]

    def body(h, g, wq, wk, wv, w_in, wo, w_out, kc, vc, lens):
        any_spec = pl.BlockSpec(memory_space=pl.ANY)
        vm = pltpu.VMEM
        dma = pltpu.SemaphoreType.DMA
        scratch = [
            vm((B, S, D), BF16), vm((B, S, D), BF16),
            vm((L, 512, 512), BF16), vm((L, 512, 512), BF16), vm((L, 512, 512), BF16), vm((L, 512, 2048), BF16),
            vm((L, 512, 512), BF16), vm((L, 2048, 512), BF16),
            vm((NY, L, D), BF16), vm((1, B), jnp.int32), vm((1, D), F32),
            vm((B, D), F32), vm((B, D), F32), vm((B, D), F32),
            vm((L, NY, B, D), BF16),
            vm((L, nch, NX * NY, 1, B), F32),
            vm((2, 3, 2, B, D), F32),
            vm((L, 2, 3, 2, B, D), BF16),
            vm((L, 3, 2, B, D), BF16),
            vm((2, 3, B, D), F32),
            vm((L, 2, 3, B, D), BF16),
            vm((L, 3, B, D), BF16),
            vm((2, B, 1024), F32),
            vm((L, 2, B, 1024), BF16),
            vm((L, B, 1024), BF16),
            vm((B, 1024), F32),
            vm((L, B, 1024), BF16),
            vm((L, B, 1024), BF16),
            vm((L, 2, B, 1024), BF16),
            vm((L, NX, B, D), BF16),
            vm((NY, B, D), F32),
            vm((L, NY, B, D), BF16),
            vm((L, NY - 1, B, D), BF16),
            vm((B, D), BF16), vm((L, B, D), BF16), vm((L, B, D), BF16), vm((B, D), BF16),
            dma((4,)), dma((L, 6)), dma((NG,)), dma((NG,)), dma((3, max(L, nch))),
            dma((L, nch, NX * NY)), dma((L, nch, NX * NY)),
            dma((L, nch, 4)), dma((L, nch, 4)), dma((4,)), dma((4,)),
            dma((L, nch, 2)), dma((L, nch, 2)), dma((L, nch, 2)), dma((L, nch, 2)),
            dma((L, nch, 2)), dma((L, nch, 2)), dma((L, nch)), dma((L, nch)),
            dma((L, nch, 3)), dma((L, nch, 3)), dma((L, nch, 4)), dma((L, nch, 4)),
        ]
        h_new, k_new, v_new = pl.pallas_call(
            functools.partial(_kernel, nch),
            out_shape=(jax.ShapeDtypeStruct((B, D), BF16), jax.ShapeDtypeStruct((L, B, D), BF16),
                       jax.ShapeDtypeStruct((L, B, D), BF16)),
            in_specs=[any_spec] * 12,
            out_specs=(any_spec,) * 3,
            scratch_shapes=scratch,
            compiler_params=pltpu.CompilerParams(collective_id=0, has_side_effects=True,
                                                 vmem_limit_bytes=67_043_328),
            name="decode_step",
        )(h, g, wq, wk, wv, w_in, wo, w_out, kc.reshape(L, B, S, D), vc.reshape(L, B, S, D),
          lens.reshape(1, B), jnp.asarray(inv_np))
        return h_new, k_new.reshape(L, B, 1, D), v_new.reshape(L, B, 1, D)

    return jax.shard_map(
        body, mesh=mesh,
        in_specs=(act, act, w_first, w_first, w_first, w_first, w_second, w_second, cache, cache, P(None)),
        out_specs=(act, new, new), check_vma=False)
```

time: 263 us -> 63.4 us (0.24)
  blocking collectives: 99.4 us -> 0 us
  waiting for transfers between devices: 80.5 us -> 0 us
  Pallas kernels: 0 us -> 58.2 us
  matrix products: 48.6 us -> 0 us
  other arithmetic: 14.3 us -> 0 us
  between operations: 14.2 us -> 0.64 us
    psum x2 -> x0, blocking collectives: 66.5 us -> none  [body(): ss = lax.psum(jnp.sum(hf * hf, axis=-1, keepdims=True), ('yz', 'x'))]
    pallas_call x0 -> x1, Pallas kernels: none -> 58.2 us  [body(): pl.pallas_call(functools.partial(_kernel, nch), out_shape=(jax.ShapeDtype...]
    dot_general x16 -> x0, matrix products: 48.6 us -> none  [the longest x2 20.4 us: _attend(): jnp.einsum('bhd,bhsd->bhs', q, kc, preferred_element_type=jnp.float32)]
    unnamed x6 -> x0, waiting for transfers between devices: 41 us -> none
    reduce_scatter x2 -> x0, waiting for transfers between devices: 39.4 us -> none  [body(): lax.psum_scatter(jnp.concatenate(parts, axis=2), 'x', scatter_dimension=1...]
    all_gather x4 -> x0, blocking collectives: 32.9 us -> none  [the longest x2 18.4 us: body(): xg = lax.all_gather(x, 'yz', axis=1, tiled=True)]
    convert_element_type x8 -> x0, other arithmetic: 5.37 us -> none  [the longest x2 2 us: body(): jax.nn.gelu(r[:, 3 * hdn:].astype(jnp.float32), approximate=True)]
    another operation x6 -> x0, other arithmetic: 3.65 us -> none  [the longest x4 2.97 us: body(): return (h, jnp.stack(ks), jnp.stack(vs))]
  transfers between devices with their start and end apart: 4 -> 0, of which waited for: 4 -> 0; matrix products, arithmetic and copies ran while one was open for 1% -> 0% of each run, Pallas kernels for 0% -> 0%
where the time goes in v1:
time: 63.4 us; the launch traced here: 63.1 us
  Pallas kernels  58.2 us (92%)
  local copies, waits for them, and re-layouts  4.32 us (7%)
  between operations  0.64 us (1%)
    pallas_call x1, Pallas kernels, body(): pl.pallas_call(functools.partial(_kernel, nch), out_shape=(jax.ShapeDtype...  58.2 us
    unnamed x3, local copies, waits for them, and re-layouts  4.32 us

profile of v1, /device:TPU:0, one launch (start us, length us, event | category | flops | bytes accessed | tf_op | source)
XLA Modules:
  0.0 63.1 jit_solution(13536113647108950241)
XLA Ops:
  0.6 58.2 %decode_step.1 = (bf16[128,128]{1,0:T(8,128)(2,1)}, bf16[2,128,128]{2,1,0:T(8,128)(2,1)}, bf16[2,128,128]{2,1,0:T(8,128)(2,1)}) custom-call(bf16[128,128]{1,0:T(8,128)(2,1)} %h_in.1, bf16[2,128]{1,0:T(2,128)(2,1)} %g_in.1, bf16[2,512,512]{2,1,0:T(8,128)(2,1)} %wq_in.1, bf16[2,512,512]{2,1,0:T(8,128)(2,1)} %wk_in.1, bf16[2,512,512]{2,1,0:T(8,128)(2,1)} %wv_in.1, ...), custom_call_target="tpu_custom_call" | custom-call | tf_op jit(solution)/shard_map/decode_step/pallas_call | solution.py:385
  58.8 1.4 %copy.20 = bf16[128,128]{1,0:T(8,128)(2,1)} copy(bf16[128,128]{1,0:T(8,128)(2,1)} %get-tuple-element.15) | data formatting | bytes 65536
  60.2 1.5 %copy.21 = bf16[2,128,1,128]{3,1,2,0:T(8,128)(2,1)} copy(bf16[2,128,1,128]{3,1,2,0:T(8,128)(2,1)} %bitcast.12) | data formatting | bytes 131072
  61.7 1.5 %copy.22 = bf16[2,128,1,128]{3,1,2,0:T(8,128)(2,1)} copy(bf16[2,128,1,128]{3,1,2,0:T(8,128)(2,1)} %bitcast.11) | data formatting | bytes 131072

commit v2 on v1

--- a/solution.py
+++ b/solution.py
@@ -35,10 +35,10 @@
 def _kernel(nch, h_in, g_in, wq_in, wk_in, wv_in, win_in, wo_in, wout_in, kc_in, vc_in, lens_in, inv_in,
             h_out, k_out, v_out,
             kbuf, vbuf, wq, wk, wv, win, wo, wout, gg, lrow, inv, cosb, sinb, lenb,
-            hg, ssb, pf, pb, rq, sf, sb, xr, uf, ub, ur, usf, usb, ux, fb, og, zf, zb, zr,
-            qv, kv, vv, hout,
+            hg, ssb, qf, qb, qr, pf, pb, rq, sf, sb, xr, uf, ub, ur, usf, usb, ux, fb, og, zf, zb, zr,
+            qv, kv, vv, hout, sbuf, pbuf, pnew, rden,
             sem_in, sem_w, sem_k, sem_v, sem_o,
-            s_send, s_recv, h_send, h_recv, g_send, g_recv, q_send, q_recv, qx_send, qx_recv,
+            s_send, s_recv, h_send, h_recv, g_send, g_recv, q_send, q_recv, kv_send, kv_recv, qx_send, qx_recv,
             u_send, u_recv, f_send, f_recv, o_send, o_recv, y_send, y_recv):
     R = B // nch
     xi = lax.axis_index("x")
@@ -144,7 +144,8 @@
                 waited.add((l, n))
                 w_cp[l, n].wait()
 
-    q_cp, u_cp, x_cp, ux_cp, f_cp, o_cp, y_cp = {}, {}, {}, {}, {}, {}, {}
+    q_cp, kv_cp, u_cp, x_cp, ux_cp, f_cp, o_cp, y_cp = {}, {}, {}, {}, {}, {}, {}, {}
+    out_cps = []
 
     def stage_in(l, ch):
         rows = pl.ds(ch * R, R)
@@ -165,20 +166,28 @@
             gj = gg[j, pl.ds(l, 1), :].astype(F32)
             xs.append((hg[l, j, rows, :].astype(F32) * r * gj).astype(BF16))
         x = jnp.concatenate(xs, axis=1)
-        for t, w in enumerate((wq, wk, wv)):
-            need_w(l, t)
+        need_w(l, 0)
+        for n in range(2):
+            acc = _dot(x, wq[l, :, pl.ds(n * 256, 256)])
+            for m in range(2):
+                a = acc[:, m * D:(m + 1) * D]
+                qf[2 * n + m, rows, :] = a
+                qb[l, 2 * n + m, rows, :] = a.astype(BF16)
+        q_cp[l, ch] = []
+        for d in (2, 1, 3):
+            to = lax.rem(xi + d, NX)
+            q_cp[l, ch].append(remote(qb.at[l, to, rows], qr.at[l, d - 1, rows], q_send.at[l, ch, d],
+                                      q_recv.at[l, ch, d], x=to))
+        for t, w in enumerate((wk, wv)):
+            need_w(l, t + 1)
             for n in range(2):
                 acc = _dot(x, w[l, :, pl.ds(n * 256, 256)])
                 for cc in range(2):
                     a = acc[:, cc * D:(cc + 1) * D]
                     pf[cc, t, n, rows, :] = a
                     pb[l, cc, t, n, rows, :] = a.astype(BF16)
-            if t == 0:
-                q_cp[l, ch, 0] = remote(pb.at[l, 1 - c, pl.ds(0, 1), :, rows], rq.at[l, pl.ds(0, 1), :, rows],
-                                        q_send.at[l, ch, 0], q_recv.at[l, ch, 0], x=partner)
-        q_cp[l, ch, 1] = remote(pb.at[l, 1 - c, pl.ds(1, 2), :, rows], rq.at[l, pl.ds(1, 2), :, rows],
-                                q_send.at[l, ch, 1], q_recv.at[l, ch, 1], x=partner)
-        reduce_qkv(l, ch, 0)
+        kv_cp[l, ch] = remote(pb.at[l, 1 - c, :, :, rows], rq.at[l, :, :, rows],
+                              kv_send.at[l, ch], kv_recv.at[l, ch], x=partner)
         need_w(l, 3)
         for n in range(8):
             acc = _dot(x, win[l, :, pl.ds(n * 256, 256)])
@@ -187,74 +196,97 @@
             ub[l, n // 4, rows, cols] = acc.astype(BF16)
         u_cp[l, ch] = remote(ub.at[l, 1 - c, rows], ur.at[l, rows], u_send.at[l, ch, 0], u_recv.at[l, ch, 0],
                              x=partner)
-        reduce_qkv(l, ch, 1)
-
-    def reduce_qkv(l, ch, part):
-        rows = pl.ds(ch * R, R)
-        ts = (0,) if part == 0 else (1, 2)
-        q_cp[l, ch, part].wait_recv()
-        for t in ts:
+
+    def reduce_kv(l, ch):
+        rows = pl.ds(ch * R, R)
+        kv_cp[l, ch].wait_recv()
+        for t in range(2):
             for n in range(2):
                 s = pf[c, t, n, rows, :] + rq[l, t, n, rows, :].astype(F32)
                 sf[n, t, rows, :] = s
                 sb[l, n, t, rows, :] = s.astype(BF16)
-        span = pl.ds(ts[0], len(ts))
-        x_cp[l, ch, part] = remote(sb.at[l, 1 - xc, span, rows], xr.at[l, span, rows],
-                                   qx_send.at[l, ch, part], qx_recv.at[l, ch, part], x=across)
-
-    def reduce_u(l, ch):
-        rows = pl.ds(ch * R, R)
-        u_cp[l, ch].wait_recv()
+        x_cp[l, ch] = remote(sb.at[l, 1 - xc, :, rows], xr.at[l, :, rows],
+                             qx_send.at[l, ch], qx_recv.at[l, ch], x=across)
+
+    def reduce_u(l, ch, piece, pieces):
+        if piece == 0:
+            u_cp[l, ch].wait_recv()
+            ux_cp[l, ch] = []
+        size = R // pieces
+        rows = pl.ds(ch * R + piece * size, size)
         us = uf[c, rows, :] + ur[l, rows, :].astype(F32)
         usf[rows, :] = us
         usb[l, rows, :] = us.astype(BF16)
-        ux_cp[l, ch] = remote(usb.at[l, rows], ux.at[l, rows], u_send.at[l, ch, 1], u_recv.at[l, ch, 1], x=across)
+        ux_cp[l, ch].append(remote(usb.at[l, rows], ux.at[l, rows], u_send.at[l, ch, 1 + piece],
+                                   u_recv.at[l, ch, 1 + piece], x=across))
 
     def rope(t, rows):
         tf = t.astype(F32)
         return (tf * cosb[rows, :] + pltpu.roll(tf, D // 2, 1) * sinb[rows, :]).astype(BF16)
 
-    def stage_qkv(l, ch):
-        rows = pl.ds(ch * R, R)
-        x_cp[l, ch, 0].wait_recv()
-        qv[rows, :] = rope((sf[xc, 0, rows, :] + xr[l, 0, rows, :].astype(F32)).astype(BF16), rows)
-        x_cp[l, ch, 1].wait_recv()
-        kv[l, rows, :] = rope((sf[xc, 1, rows, :] + xr[l, 1, rows, :].astype(F32)).astype(BF16), rows)
-        vv[l, rows, :] = (sf[xc, 2, rows, :] + xr[l, 2, rows, :].astype(F32)).astype(BF16)
+    def stage_q(l, ch):
+        rows = pl.ds(ch * R, R)
+        for cp in q_cp[l, ch]:
+            cp.wait_recv()
+        q = qf[xi, rows, :]
+        for d in range(NX - 1):
+            q = q + qr[l, d, rows, :].astype(F32)
+        qv[rows, :] = rope(q.astype(BF16), rows)
+
+    def stage_kv(l, ch):
+        rows = pl.ds(ch * R, R)
+        x_cp[l, ch].wait_recv()
+        kv[l, rows, :] = rope((sf[xc, 0, rows, :] + xr[l, 0, rows, :].astype(F32)).astype(BF16), rows)
+        vv[l, rows, :] = (sf[xc, 1, rows, :] + xr[l, 1, rows, :].astype(F32)).astype(BF16)
+        out_cps.append(load(kv.at[l, rows], k_out.at[l, rows], sem_o.at[l, 0, ch]))
+        out_cps.append(load(vv.at[l, rows], v_out.at[l, rows], sem_o.at[l, 1, ch]))
 
     rowid = lax.broadcasted_iota(jnp.int32, (G, D), 0)
-    pos = lax.broadcasted_iota(jnp.int32, (G, S), 1).astype(F32)
+    pos = lax.broadcasted_iota(jnp.int32, (R, S), 1).astype(F32)
     scale = D ** -0.5
-
-    def attend(l, g0, g1):
-        @pl.loop(g0, g1)
+    gpc = NG // nch
+
+    def scores(l, ch):
+        @pl.loop(ch * gpc, (ch + 1) * gpc)
         def _(grp):
             base = grp * G
             rows = pl.ds(base, G)
             pltpu.make_async_copy(kc_in.at[l, rows], kbuf.at[rows], sem_k.at[grp]).wait()
-            pltpu.make_async_copy(vc_in.at[l, rows], vbuf.at[rows], sem_v.at[grp]).wait()
-            qf = qv[rows, :].astype(F32)
+            q = qv[rows, :].astype(F32)
             s = jnp.zeros((G, S), F32)
             for i in range(0, G, 2):
-                lhs = jnp.concatenate([jnp.where(rowid == i, qf, 0.0), jnp.where(rowid == i + 1, qf, 0.0)],
+                lhs = jnp.concatenate([jnp.where(rowid == i, q, 0.0), jnp.where(rowid == i + 1, q, 0.0)],
                                       axis=1).astype(BF16)
                 s = s + _dot_t(lhs, jnp.concatenate([kbuf[base + i], kbuf[base + i + 1]], axis=1))
-            s = jnp.where(pos < lenb[rows, :][:, :1], s * scale, -jnp.inf)
-            kf = kv[l, rows, :].astype(F32)
-            vf = vv[l, rows, :].astype(F32)
-            s_new = jnp.sum(qf * kf, axis=1, keepdims=True) * scale
-            m = jnp.maximum(jnp.max(s, axis=1, keepdims=True), s_new)
-            p = jnp.exp(s - m)
-            p_new = jnp.exp(s_new - m)
-            den = jnp.sum(p, axis=1, keepdims=True) + p_new
-            p = p.astype(BF16)
-            o = p_new * vf
+            sbuf[rows, :] = s
+            if l + 1 < L:
+                pltpu.make_async_copy(kc_in.at[l + 1, rows], kbuf.at[rows], sem_k.at[grp]).start()
+
+    def softmax(l, ch):
+        rows = pl.ds(ch * R, R)
+        s = jnp.where(pos < lenb[rows, :][:, :1], sbuf[rows, :] * scale, -jnp.inf)
+        s_new = jnp.sum(qv[rows, :].astype(F32) * kv[l, rows, :].astype(F32), axis=1, keepdims=True) * scale
+        m = jnp.maximum(jnp.max(s, axis=1, keepdims=True), s_new)
+        p = jnp.exp(s - m)
+        p_new = jnp.exp(s_new - m)
+        pbuf[rows, :] = p.astype(BF16)
+        pnew[rows, :] = p_new * vv[l, rows, :].astype(F32)
+        rden[rows, :] = jnp.broadcast_to(jnp.sum(p, axis=1, keepdims=True) + p_new, (R, D))
+
+    def values(l, ch):
+        @pl.loop(ch * gpc, (ch + 1) * gpc)
+        def _(grp):
+            base = grp * G
+            rows = pl.ds(base, G)
+            pltpu.make_async_copy(vc_in.at[l, rows], vbuf.at[rows], sem_v.at[grp]).wait()
+            p = pbuf[rows, :]
+            o = pnew[rows, :]
             for i in range(0, G, 2):
                 t = _dot(p, jnp.concatenate([vbuf[base + i], vbuf[base + i + 1]], axis=1))
                 o = o + jnp.where(rowid == i, t[:, :D], jnp.where(rowid == i + 1, t[:, D:], 0.0))
-            og[l, xi, rows, :] = (o / den).astype(BF16)
+            og[l, xi, rows, :] = (o / rden[rows, :]).astype(BF16)
             if l + 1 < L:
-                load_cache(l + 1, grp)
+                pltpu.make_async_copy(vc_in.at[l + 1, rows], vbuf.at[rows], sem_v.at[grp]).start()
 
     def send_o(l, ch):
         rows = pl.ds(ch * R, R)
@@ -263,7 +295,8 @@
 
     def stage_f(l, ch):
         rows = pl.ds(ch * R, R)
-        ux_cp[l, ch].wait_recv()
+        for cp in ux_cp[l, ch]:
+            cp.wait_recv()
         u = (usf[rows, :] + ux[l, rows, :].astype(F32)).astype(BF16)
         fb[l, c, rows, :] = jax.nn.gelu(u.astype(F32), approximate=True).astype(BF16)
         f_cp[l, ch] = remote(fb.at[l, c, rows], fb.at[l, c, rows], f_send.at[l, ch], f_recv.at[l, ch], x=partner)
@@ -295,8 +328,6 @@
             y_cp[l, ch].append(remote(zb.at[l, to, rows], zr.at[l, d - 1, rows], y_send.at[l, ch, d],
                                       y_recv.at[l, ch, d], yz=to))
 
-    out_cps = []
-
     def stage_h(l, ch):
         rows = pl.ds(ch * R, R)
         for cp in y_cp[l, ch]:
@@ -311,24 +342,36 @@
             send_h(l + 1, ch)
         else:
             hout[rows, :] = hn
-            out_cps.append(load(hout.at[rows], h_out.at[rows], sem_o.at[0, ch]))
-
-    gpc = NG // nch
+            out_cps.append(load(hout.at[rows], h_out.at[rows], sem_o.at[l, 2, ch]))
+
     for l in range(L):
-        for ch in range(nch):
-            stage_in(l, ch)
-            reduce_u(l, ch)
-            stage_qkv(l, ch)
-        out_cps.append(load(kv.at[l], k_out.at[l], sem_o.at[1, l]))
-        out_cps.append(load(vv.at[l], v_out.at[l], sem_o.at[2, l]))
-        for ch in range(nch):
-            attend(l, ch * gpc, (ch + 1) * gpc)
-            send_o(l, ch)
-            stage_f(l, ch)
-            stage_mlp(l, ch)
-            stage_out(l, ch)
-        for ch in range(nch):
-            stage_h(l, ch)
+        stage_in(l, 0)
+        reduce_kv(l, 0)
+        reduce_u(l, 0, 0, 1)
+        stage_in(l, 1)
+        reduce_kv(l, 1)
+        reduce_u(l, 1, 0, 2)
+        stage_q(l, 0)
+        scores(l, 0)
+        stage_kv(l, 0)
+        softmax(l, 0)
+        values(l, 0)
+        send_o(l, 0)
+        reduce_u(l, 1, 1, 2)
+        stage_q(l, 1)
+        scores(l, 1)
+        stage_kv(l, 1)
+        softmax(l, 1)
+        stage_f(l, 0)
+        values(l, 1)
+        send_o(l, 1)
+        stage_mlp(l, 0)
+        stage_out(l, 0)
+        stage_f(l, 1)
+        stage_mlp(l, 1)
+        stage_out(l, 1)
+        stage_h(l, 0)
+        stage_h(l, 1)
     for cp in out_cps:
         cp.wait()
     for cp in sends:
@@ -336,7 +379,7 @@
 
 
 def solution(mesh):
-    nch = 1
+    nch = 2
     act = P(None, ('x', 'yz'))
     w_first = P(None, 'x', 'yz')
     w_second = P(None, 'yz', 'x')
@@ -357,12 +400,15 @@
             vm((B, D), F32), vm((B, D), F32), vm((B, D), F32),
             vm((L, NY, B, D), BF16),
             vm((L, nch, NX * NY, 1, B), F32),
-            vm((2, 3, 2, B, D), F32),
-            vm((L, 2, 3, 2, B, D), BF16),
-            vm((L, 3, 2, B, D), BF16),
-            vm((2, 3, B, D), F32),
-            vm((L, 2, 3, B, D), BF16),
-            vm((L, 3, B, D), BF16),
+            vm((NX, B, D), F32),
+            vm((L, NX, B, D), BF16),
+            vm((L, NX - 1, B, D), BF16),
+            vm((2, 2, 2, B, D), F32),
+            vm((L, 2, 2, 2, B, D), BF16),
+            vm((L, 2, 2, B, D), BF16),
+            vm((2, 2, B, D), F32),
+            vm((L, 2, 2, B, D), BF16),
+            vm((L, 2, B, D), BF16),
             vm((2, B, 1024), F32),
             vm((L, 2, B, 1024), BF16),
             vm((L, B, 1024), BF16),
@@ -375,11 +421,12 @@
             vm((L, NY, B, D), BF16),
             vm((L, NY - 1, B, D), BF16),
             vm((B, D), BF16), vm((L, B, D), BF16), vm((L, B, D), BF16), vm((B, D), BF16),
-            dma((4,)), dma((L, 6)), dma((NG,)), dma((NG,)), dma((3, max(L, nch))),
+            vm((B, S), F32), vm((B, S), BF16), vm((B, D), F32), vm((B, D), F32),
+            dma((4,)), dma((L, 6)), dma((NG,)), dma((NG,)), dma((L, 3, nch)),
             dma((L, nch, NX * NY)), dma((L, nch, NX * NY)),
             dma((L, nch, 4)), dma((L, nch, 4)), dma((4,)), dma((4,)),
-            dma((L, nch, 2)), dma((L, nch, 2)), dma((L, nch, 2)), dma((L, nch, 2)),
-            dma((L, nch, 2)), dma((L, nch, 2)), dma((L, nch)), dma((L, nch)),
+            dma((L, nch, 4)), dma((L, nch, 4)), dma((L, nch)), dma((L, nch)), dma((L, nch)), dma((L, nch)),
+            dma((L, nch, 3)), dma((L, nch, 3)), dma((L, nch)), dma((L, nch)),
             dma((L, nch, 3)), dma((L, nch, 3)), dma((L, nch, 4)), dma((L, nch, 4)),
         ]
         h_new, k_new, v_new = pl.pallas_call(

time: 63.4 us -> 59.7 us (0.942)
  Pallas kernels: 58.2 us -> 54.5 us
    pallas_call x1, Pallas kernels: 58.2 us -> 54.5 us  [body(): pl.pallas_call(functools.partial(_kernel, nch), out_shape=(jax.ShapeDtype...]
where the time goes in v2:
time: 59.7 us; the launch traced here: 59.5 us
  Pallas kernels  54.5 us (91%)
  local copies, waits for them, and re-layouts  4.32 us (7%)
  between operations  0.64 us (1%)
    pallas_call x1, Pallas kernels, body(): pl.pallas_call(functools.partial(_kernel, nch), out_shape=(jax.ShapeDtype...  54.5 us
    unnamed x3, local copies, waits for them, and re-layouts  4.32 us

profile of v2, /device:TPU:0, one launch (start us, length us, event | category | flops | bytes accessed | tf_op | source)
XLA Modules:
  0.0 59.5 jit_solution(13572925073349570045)
XLA Ops:
  0.6 54.5 %decode_step.1 = (bf16[128,128]{1,0:T(8,128)(2,1)}, bf16[2,128,128]{2,1,0:T(8,128)(2,1)}, bf16[2,128,128]{2,1,0:T(8,128)(2,1)}) custom-call(bf16[128,128]{1,0:T(8,128)(2,1)} %h_in.1, bf16[2,128]{1,0:T(2,128)(2,1)} %g_in.1, bf16[2,512,512]{2,1,0:T(8,128)(2,1)} %wq_in.1, bf16[2,512,512]{2,1,0:T(8,128)(2,1)} %wk_in.1, bf16[2,512,512]{2,1,0:T(8,128)(2,1)} %wv_in.1, ...), custom_call_target="tpu_custom_call" | custom-call | tf_op jit(solution)/shard_map/decode_step/pallas_call | solution.py:432
  55.1 1.4 %copy.20 = bf16[128,128]{1,0:T(8,128)(2,1)} copy(bf16[128,128]{1,0:T(8,128)(2,1)} %get-tuple-element.15) | data formatting | bytes 65536
  56.5 1.5 %copy.21 = bf16[2,128,1,128]{3,1,2,0:T(8,128)(2,1)} copy(bf16[2,128,1,128]{3,1,2,0:T(8,128)(2,1)} %bitcast.12) | data formatting | bytes 131072
  58.0 1.5 %copy.22 = bf16[2,128,1,128]{3,1,2,0:T(8,128)(2,1)} copy(bf16[2,128,1,128]{3,1,2,0:T(8,128)(2,1)} %bitcast.11) | data formatting | bytes 131072
